TPU v7x, 32 devices: a whole 2x2x4 slice. The times are simulated.
32 devices in a mesh: node: 8 (over y, x, core), chip: 4 (over z).
Axes of the slice: x: 2, y: 2, z: 4, core: 2. Of those that a mesh axis runs over, the one named last changes fastest.
Arguments:
- momentum: float32 [32, 128, 512], P(('node', 'chip')), may hold values from -6 to 6
- gradient: bfloat16 [32, 128, 512], P(('node', 'chip')), may hold values from -6 to 6
- indices: int32 [32, 16, 32], P(('node', 'chip')), may hold values from 0 to 4095, as said below
Outputs:
- new_momentum: float32 [32, 128, 512], P(('node', 'chip'))
- update: float32 [128, 512], replicated
Inputs may be any that keep to these rules, and one draw needn't show every extreme that they name: `indices`: the 32 entries of each row name distinct coefficients of their span, coefficient (k, l) being k * 64 + l.
All inputs are finite; a program needn't handle non-finite values.
Results may differ from a plain program's by a relative error of at most 0.0029.
Values may be sent and summed in bfloat16 or wider, within the bound.
A program may use at most 64 MiB of HBM per device.

v0:
```python
import math
import jax
import jax.numpy as jnp
from jax import lax
from jax.sharding import PartitionSpec as P

SPAN = 64


def dct_table(edge_len):
    orders = jnp.arange(edge_len, dtype=jnp.float32)
    wave_no = orders[:, None]
    cell_no = orders[None, :]
    factor = jnp.where(wave_no == 0.0, math.sqrt(1.0 / edge_len), math.sqrt(2.0 / edge_len))
    return factor * jnp.cos(math.pi * (2.0 * cell_no + 1.0) * wave_no / (2.0 * edge_len))


def forward(grid_field, cosines, edge_len):
    row_blocks = grid_field.shape[0] // edge_len
    col_blocks = grid_field.shape[1] // edge_len
    blocks = grid_field.reshape(row_blocks, edge_len, col_blocks, edge_len).transpose(0, 2, 1, 3)
    coeffs = jnp.einsum(
        "kn,abnm,lm->abkl", cosines, blocks, cosines, precision=lax.Precision.HIGHEST
    )
    return coeffs.reshape(row_blocks * col_blocks, edge_len * edge_len)


def inverse_blocks(coeffs, cosines, edge_len):
    blocks = coeffs.reshape(coeffs.shape[0], edge_len, edge_len)
    return jnp.einsum("kn,ckl,lm->cnm", cosines, blocks, cosines, precision=lax.Precision.HIGHEST)


def place_blocks(blocks, row_count, col_count, edge_len):
    shaped = blocks.reshape(row_count // edge_len, col_count // edge_len, edge_len, edge_len)
    return shaped.transpose(0, 2, 1, 3).reshape(row_count, col_count)


def normalized(blocks):
    energy = jnp.mean(blocks * blocks, axis=(1, 2), keepdims=True)
    return blocks / jnp.sqrt(energy + 1.0)


def decode_block(picked, slots):
    n_spans = picked.shape[1]
    values_rows = jnp.moveaxis(picked, 1, 0).reshape(n_spans, -1)
    slot_rows = jnp.moveaxis(slots, 1, 0).reshape(n_spans, -1)
    orders = jnp.arange(SPAN, dtype=jnp.int32)[None, :]

    def one_span(pair):
        vals, where = pair
        wave_rows = (where // SPAN)[:, None] == orders
        wave_cols = (where % SPAN)[:, None] == orders
        left_hot = wave_rows.astype(jnp.bfloat16)
        right_hot = jnp.where(wave_cols, vals[:, None], jnp.zeros((), jnp.bfloat16))
        block = lax.dot_general(
            left_hot, right_hot, (((0,), (0,)), ((), ())), preferred_element_type=jnp.float32
        )
        return block.reshape(SPAN * SPAN)

    return lax.map(one_span, (values_rows, slot_rows))


def decode_lists(totals, picked, slots):
    count = picked.shape[0]
    group_len = 1
    for trial in range(1, 17):
        if count % trial == 0:
            group_len = trial
    picked_groups = picked.reshape((count // group_len, group_len) + picked.shape[1:])
    slot_groups = slots.reshape((count // group_len, group_len) + slots.shape[1:])

    def add_group(step, carry):
        return carry + decode_block(picked_groups[step], slot_groups[step])

    return lax.fori_loop(0, count // group_len, add_group, totals)


def shards(momentum, gradient, indices):
    cosines = dct_table(SPAN)
    row_count = momentum.shape[1]
    col_count = momentum.shape[2]
    blended = 0.9 * momentum[0] + gradient[0].astype(jnp.float32)
    coeffs = forward(blended, cosines, SPAN)
    slots = indices[0]
    picked = jnp.take_along_axis(coeffs, slots, axis=1).astype(jnp.bfloat16)
    sparse = decode_block(picked[None], indices)
    own_part = place_blocks(inverse_blocks(sparse, cosines, SPAN), row_count, col_count, SPAN)
    new_momentum = (blended - own_part)[None]
    partial_sum = decode_lists(
        jnp.zeros_like(coeffs),
        lax.all_gather(picked[None], "chip", axis=0, tiled=True),
        lax.all_gather(indices, "chip", axis=0, tiled=True),
    )
    totals = lax.psum(partial_sum, "node")
    update = place_blocks(
        normalized(inverse_blocks(totals, cosines, SPAN)), row_count, col_count, SPAN
    )
    return (new_momentum, update)


def solution(mesh):
    return jax.shard_map(
        shards,
        mesh=mesh,
        in_specs=(
            P(("node", "chip"), None, None),
            P(("node", "chip"), None, None),
            P(("node", "chip"), None, None),
        ),
        out_specs=(P(("node", "chip"), None, None), P()),
        check_vma=False,
    )
```

profile of v0, /device:TPU:0, one launch (start us, length us, event | category | flops | bytes accessed | tf_op | source)
XLA Modules:
  0.0 127.8 jit_solution(4356147614158876346)
XLA Ops:
  7.2 0.8 fusion.53
  8.0 14.8 %all_gather.6 = s32[4,16,32]{2,1,0:T(8,128)S(1)} all-gather(s32[1,16,32]{2,1,0:T(8,128)S(1)} %copy-done), channel_id=1, replica_groups=mesh['node'=8,'chip'=4] {'chip'}, dimensions={0}, use_global_device_ids=true | all-gather | bytes 10240 | tf_op jit(solution)/shard_map/all_gather | solution.py:92
  22.8 1.1 convert_add_fusion
  24.3 1.7 %fusion.20 = f32[2,8,64,64]{2,3,1,0:T(8,128)S(1)} fusion(f32[2,64,8,64]{1,3,2,0:T(8,128)S(1)} %copy.20, f32[64]{0:T(128)S(1)} %get-tuple-element.232, f32[64]{0:T(128)S(1)} %get-tuple-element.231), kind=kOutput, calls=%fused_computation.37 | convolution fusion | flops 50343936 | bytes 524800 | tf_op jit(solution)/shard_map/kn,abnm,lm->abkl/dot_general | solution.py:22
  26.0 0.7 fusion.22
  27.0 4.8 %gather_fusion = bf16[512]{0:T(512)(128)(2,1)S(1)} fusion(bf16[16,4096]{1,0:T(8,128)(2,1)S(1)} %reshape.216, s32[512]{0:T(512)S(1)} %reshape.225), kind=kCustom, calls=%fused_computation | custom fusion | bytes 6144 | tf_op jit(solution)/shard_map/jit(take_along_axis)/gather | solution.py:85
  32.0 13.2 %all_gather.7 = bf16[4,16,32]{2,1,0:T(8,128)(2,1)S(1)} all-gather(bf16[1,16,32]{2,1,0:T(8,128)(2,1)S(1)} %select_convert_fusion), channel_id=1, replica_groups=mesh['node'=8,'chip'=4] {'chip'}, dimensions={0}, use_global_device_ids=true | all-gather | bytes 5120 | tf_op jit(solution)/shard_map/all_gather | solution.py:91
  45.4 13.3 %while.37 = (s32[]{:T(128)}, f32[16,4096]{1,0:T(8,128)S(1)}, s32[16,128]{1,0:T(8,128)S(1)}, bf16[16,128]{1,0:T(8,128)(2,1)S(1)}, s32[]{:T(128)}, /*index=5*/s32[]{:T(128)}) while((s32[]{:T(128)}, f32[16,4096]{1,0:T(8,128)S(1)}, s32[16,128]{1,0:T(8,128)S(1)}, bf16[16,128]{1,0:T(8,128)(2,1)S(1)}, s32[]{:T(128)}, ...), condition=%wide.region_3.4_spmd.clone.clone, body=%wide.region_2.3_spmd.clone.clone.sunk | while | flops 1075714 | bytes 86353 | solution.py:60
  45.8 0.4 dynamic_update_slice.20
  46.7 0.4 dynamic_update_slice.20
  47.5 0.4 dynamic_update_slice.20
  48.3 0.4 dynamic_update_slice.20
  49.2 0.4 dynamic_update_slice.20
  50.0 0.4 dynamic_update_slice.20
  50.8 0.4 dynamic_update_slice.20
  51.7 0.4 dynamic_update_slice.20
  52.5 0.4 dynamic_update_slice.20
  53.3 0.4 dynamic_update_slice.20
  54.1 0.4 dynamic_update_slice.20
  55.0 0.4 dynamic_update_slice.20
  55.8 0.4 dynamic_update_slice.20
  56.6 0.4 dynamic_update_slice.20
  57.5 0.4 dynamic_update_slice.20
  58.3 0.4 dynamic_update_slice.20
  58.9 1.0 copy.27
  60.1 13.3 %while.36 = (s32[]{:T(128)}, f32[16,4096]{1,0:T(8,128)S(1)}, s32[16,32]{1,0:T(8,128)S(1)}, bf16[16,32]{1,0:T(8,128)(2,1)S(1)}, s32[]{:T(128)}, /*index=5*/s32[]{:T(128)}) while((s32[]{:T(128)}, f32[16,4096]{1,0:T(8,128)S(1)}, s32[16,32]{1,0:T(8,128)S(1)}, bf16[16,32]{1,0:T(8,128)(2,1)S(1)}, s32[]{:T(128)}, ...), condition=%wide.region_1.2_spmd.clone.clone, body=%wide.region_0.1_spmd.clone.clone.sunk | while | flops 268930 | bytes 83089 | solution.py:60
  60.5 0.4 dynamic_update_slice.19
  61.3 0.4 dynamic_update_slice.19
  62.2 0.4 dynamic_update_slice.19
  63.0 0.4 dynamic_update_slice.19
  63.8 0.4 dynamic_update_slice.19
  64.7 0.4 dynamic_update_slice.19
  65.5 0.4 dynamic_update_slice.19
  66.3 0.4 dynamic_update_slice.19
  67.2 0.4 dynamic_update_slice.19
  68.0 0.4 dynamic_update_slice.19
  68.8 0.4 dynamic_update_slice.19
  69.7 0.4 dynamic_update_slice.19
  70.5 0.4 dynamic_update_slice.19
  72.2 0.4 dynamic_update_slice.19
  73.0 0.4 dynamic_update_slice.19
  73.6 0.7 fusion.31
  74.4 0.7 fusion.29
  75.5 0.7 sub.16
  76.3 39.7 %all-reduce.2.cloned.1.call-done = f32[16,64,64]{1,2,0:T(8,128)} async-done(((f32[16,64,64]{1,2,0:T(8,128)}), f32[16,64,64]{1,2,0:T(8,128)}) %all-reduce.2.cloned.1.call-update) | async-done | bytes 262160 | tf_op jit(solution)/shard_map/psum | solution.py:94
  116.0 2.8 %fusion.27 = f32[16,64,64]{1,2,0:T(8,128)S(1)} fusion(f32[16,64,64]{1,2,0:T(8,128)} %all-reduce.2.cloned.1.call-done, f32[64]{0:T(128)S(1)} %get-tuple-element.232, f32[64]{0:T(128)S(1)} %get-tuple-element.231), kind=kOutput, calls=%fused_computation.47 | convolution fusion | flops 50343936 | bytes 524800 | tf_op jit(solution)/shard_map/kn,ckl,lm->cnm/dot_general | solution.py:30
  118.8 0.8 multiply_reduce_fusion
  120.1 0.9 reshape.224
  (187 shorter events, 15.3 us)
Async XLA Ops:
  7.2 108.9 %all-reduce.2.cloned.1.call-start = ((), (), s32[]{:S(2)}) async-start(), calls=%async_computation | async-start | bytes 1048576 | tf_op jit(solution)/shard_map/psum | solution.py:94
  7.2 0.8 copy-start
Sparse Core Ops, SparseCore 0:
  60.1 55.8 all-reduce.1
where the time goes:
time: 128 us
  waiting for transfers between devices  39.8 us (31%)
  blocking collectives  28 us (22%)
  local copies, waits for them, and re-layouts  24.9 us (19%)
  matrix products  15.8 us (12%)
  between operations  14.2 us (11%)
  other arithmetic  3.41 us (3%)
  loops' own time  1.61 us (1%)
    psum x1, waiting for transfers between devices, shards(): totals = lax.psum(partial_sum, 'node')  39.7 us
    all_gather x1, blocking collectives, shards(): lax.all_gather(indices, 'chip', axis=0, tiled=True)  14.8 us
    all_gather x1, blocking collectives, shards(): lax.all_gather(picked[None], 'chip', axis=0, tiled=True)  13.2 us
    dynamic_update_slice x32, local copies, waits for them, and re-layouts, decode_block(): return lax.map(one_span, (values_rows, slot_rows))  12.6 us
    dot_general x32, matrix products, one_span(): lax.dot_general(left_hot, right_hot, (((0,), (0,)), ((), ())), preferred_...  8.39 us
    gather x4, local copies, waits for them, and re-layouts, shards(): picked = jnp.take_along_axis(coeffs, slots, axis=1).astype(jnp.bfloat16)  5.09 us
    dot_general x4, matrix products, inverse_blocks(): jnp.einsum('kn,ckl,lm->cnm', cosines, blocks, cosines, precision=lax.Prec...  5.02 us
    broadcast_in_dim x32, local copies, waits for them, and re-layouts, decode_block(): return lax.map(one_span, (values_rows, slot_rows))  2.91 us
  transfers between devices with their start and end apart: 1, of which 1 were waited for; matrix products, arithmetic and copies ran while one was open for 12% of the time, Pallas kernels for 0%

commit v1 on v0

--- a/solution.py
+++ b/solution.py
@@ -91,7 +91,7 @@
         lax.all_gather(picked[None], "chip", axis=0, tiled=True),
         lax.all_gather(indices, "chip", axis=0, tiled=True),
     )
-    totals = lax.psum(partial_sum, "node")
+    totals = jnp.sum(lax.all_gather(partial_sum, "node"), axis=0)
     update = place_blocks(
         normalized(inverse_blocks(totals, cosines, SPAN)), row_count, col_count, SPAN
     )

time: 128 us -> 100 us (0.78)
  waiting for transfers between devices: 39.8 us -> 12.6 us
  matrix products: 15.8 us -> 13.8 us
  other arithmetic: 3.41 us -> 5.06 us
    psum x1 -> x0, waiting for transfers between devices: 39.7 us -> none  [shards(): totals = lax.psum(partial_sum, 'node')]
    all_gather x0 -> x1, waiting for transfers between devices: none -> 12.6 us  [shards(): totals = jnp.sum(lax.all_gather(partial_sum, 'node'), axis=0)]
    dot_general x4, matrix products: 5.02 us -> 2.98 us  [inverse_blocks(): jnp.einsum('kn,ckl,lm->cnm', cosines, blocks, cosines, precision=lax.Prec...]
    reduce_sum x0 -> x1, other arithmetic: none -> 1.72 us  [shards(): totals = jnp.sum(lax.all_gather(partial_sum, 'node'), axis=0)]
  transfers between devices with their start and end apart: 1 -> 1, of which waited for: 1 -> 1; matrix products, arithmetic and copies ran while one was open for 12% -> 15% of each run, Pallas kernels for 0% -> 0%
where the time goes in v1:
time: 100 us
  blocking collectives  28.3 us (28%)
  local copies, waits for them, and re-layouts  24.6 us (25%)
  between operations  14.2 us (14%)
  matrix products  13.8 us (14%)
  waiting for transfers between devices  12.6 us (13%)
  other arithmetic  5.06 us (5%)
  loops' own time  1.61 us (2%)
    all_gather x1, blocking collectives, shards(): lax.all_gather(indices, 'chip', axis=0, tiled=True)  15 us
    all_gather x1, blocking collectives, shards(): lax.all_gather(picked[None], 'chip', axis=0, tiled=True)  13.2 us
    all_gather x1, waiting for transfers between devices, shards(): totals = jnp.sum(lax.all_gather(partial_sum, 'node'), axis=0)  12.6 us
    dynamic_update_slice x32, local copies, waits for them, and re-layouts, decode_block(): return lax.map(one_span, (values_rows, slot_rows))  12.6 us
    dot_general x32, matrix products, one_span(): lax.dot_general(left_hot, right_hot, (((0,), (0,)), ((), ())), preferred_...  8.39 us
    gather x4, local copies, waits for them, and re-layouts, shards(): picked = jnp.take_along_axis(coeffs, slots, axis=1).astype(jnp.bfloat16)  5.09 us
    dot_general x4, matrix products, inverse_blocks(): jnp.einsum('kn,ckl,lm->cnm', cosines, blocks, cosines, precision=lax.Prec...  2.98 us
    broadcast_in_dim x32, local copies, waits for them, and re-layouts, decode_block(): return lax.map(one_span, (values_rows, slot_rows))  2.92 us
  transfers between devices with their start and end apart: 1, of which 1 were waited for; matrix products, arithmetic and copies ran while one was open for 15% of the time, Pallas kernels for 0%

profile of v1, /device:TPU:0, one launch (start us, length us, event | category | flops | bytes accessed | tf_op | source)
XLA Modules:
  0.0 100.2 jit_solution(13104030577230518320)
XLA Ops:
  7.2 0.7 fusion.53
  7.9 15.0 %all_gather.12 = s32[4,16,32]{2,1,0:T(8,128)S(1)} all-gather(s32[1,16,32]{2,1,0:T(8,128)} %param.9), channel_id=1, replica_groups=mesh['node'=8,'chip'=4] {'chip'}, dimensions={0}, use_global_device_ids=true | all-gather | bytes 10240 | tf_op jit(solution)/shard_map/all_gather | solution.py:92
  23.0 1.1 %convert_add_fusion = f32[1,128,512]{2,1,0:T(8,128)S(1)} fusion(bf16[1,128,512]{2,1,0:T(8,128)(2,1)} %param.8, f32[1,128,512]{2,1,0:T(8,128)} %param.7), kind=kLoop, calls=%fused_computation.41 | loop fusion | flops 196608 | bytes 655360 | tf_op jit(solution)/shard_map/add | solution.py:82
  24.4 1.7 %fusion.20 = f32[2,8,64,64]{2,3,1,0:T(8,128)S(1)} fusion(f32[2,64,8,64]{1,3,2,0:T(8,128)S(1)} %copy.20, f32[64]{0:T(128)S(1)} %get-tuple-element.232, f32[64]{0:T(128)S(1)} %get-tuple-element.231), kind=kOutput, calls=%fused_computation.37 | convolution fusion | flops 50343936 | bytes 524800 | tf_op jit(solution)/shard_map/kn,abnm,lm->abkl/dot_general | solution.py:22
  26.1 0.7 fusion.22
  27.3 4.8 %gather_fusion = bf16[512]{0:T(512)(128)(2,1)S(1)} fusion(bf16[16,4096]{1,0:T(8,128)(2,1)S(1)} %reshape.216, s32[512]{0:T(512)S(1)} %reshape.225), kind=kCustom, calls=%fused_computation | custom fusion | bytes 6144 | tf_op jit(solution)/shard_map/jit(take_along_axis)/gather | solution.py:85
  32.2 13.2 %all_gather.13 = bf16[4,16,32]{2,1,0:T(8,128)(2,1)S(1)} all-gather(bf16[1,16,32]{2,1,0:T(8,128)(2,1)S(1)} %select_convert_fusion), channel_id=1, replica_groups=mesh['node'=8,'chip'=4] {'chip'}, dimensions={0}, use_global_device_ids=true | all-gather | bytes 5120 | tf_op jit(solution)/shard_map/all_gather | solution.py:91
  45.5 13.3 %while.37 = (s32[]{:T(128)}, f32[16,4096]{1,0:T(8,128)S(1)}, s32[16,128]{1,0:T(8,128)S(1)}, bf16[16,128]{1,0:T(8,128)(2,1)S(1)}, s32[]{:T(128)}, /*index=5*/s32[]{:T(128)}) while((s32[]{:T(128)}, f32[16,4096]{1,0:T(8,128)S(1)}, s32[16,128]{1,0:T(8,128)S(1)}, bf16[16,128]{1,0:T(8,128)(2,1)S(1)}, s32[]{:T(128)}, ...), condition=%wide.region_3.4_spmd.clone.clone, body=%wide.region_2.3_spmd.clone.clone.sunk | while | flops 1075714 | bytes 86361 | solution.py:60
  46.0 0.4 dynamic_update_slice.20
  46.8 0.4 dynamic_update_slice.20
  47.6 0.4 dynamic_update_slice.20
  48.5 0.4 dynamic_update_slice.20
  49.3 0.4 dynamic_update_slice.20
  50.1 0.4 dynamic_update_slice.20
  51.0 0.4 dynamic_update_slice.20
  51.8 0.4 dynamic_update_slice.20
  52.6 0.4 dynamic_update_slice.20
  53.5 0.4 dynamic_update_slice.20
  54.3 0.4 dynamic_update_slice.20
  55.1 0.4 dynamic_update_slice.20
  56.0 0.4 dynamic_update_slice.20
  56.8 0.4 dynamic_update_slice.20
  57.6 0.4 dynamic_update_slice.20
  58.5 0.4 dynamic_update_slice.20
  58.9 0.7 copy-done
  59.7 13.3 %while.36 = (s32[]{:T(128)}, f32[16,4096]{1,0:T(8,128)S(1)}, s32[16,32]{1,0:T(8,128)S(1)}, bf16[16,32]{1,0:T(8,128)(2,1)S(1)}, s32[]{:T(128)}, /*index=5*/s32[]{:T(128)}) while((s32[]{:T(128)}, f32[16,4096]{1,0:T(8,128)S(1)}, s32[16,32]{1,0:T(8,128)S(1)}, bf16[16,32]{1,0:T(8,128)(2,1)S(1)}, s32[]{:T(128)}, ...), condition=%wide.region_1.2_spmd.clone.clone, body=%wide.region_0.1_spmd.clone.clone.sunk | while | flops 268930 | bytes 83097 | solution.py:60
  60.1 0.4 dynamic_update_slice.19
  61.0 0.4 dynamic_update_slice.19
  61.8 0.4 dynamic_update_slice.19
  62.6 0.4 dynamic_update_slice.19
  63.5 0.4 dynamic_update_slice.19
  64.3 0.4 dynamic_update_slice.19
  65.1 0.4 dynamic_update_slice.19
  66.0 0.4 dynamic_update_slice.19
  66.8 0.4 dynamic_update_slice.19
  67.6 0.4 dynamic_update_slice.19
  68.5 0.4 dynamic_update_slice.19
  70.1 0.4 dynamic_update_slice.19
  71.0 0.4 dynamic_update_slice.19
  71.8 0.4 dynamic_update_slice.19
  73.3 0.7 fusion.31
  74.0 0.7 fusion.29
  75.2 0.7 sub.16
  75.9 12.6 %all-gather.3.cloned.1.call-done = f32[128,4096]{1,0:T(8,128)} async-done(((f32[16,4096]{1,0:T(8,128)}), f32[128,4096]{1,0:T(8,128)}) %all-gather.3.cloned.1.call-update) | async-done | bytes 2097168 | tf_op jit(solution)/shard_map/all_gather | solution.py:94
  88.5 1.7 %reduce_sum.18 = f32[16,4096]{1,0:T(8,128)S(1)} reduce(f32[8,16,4096]{2,1,0:T(8,128)} %bitcast.83, f32[]{:T(128)} %constant.162.clone.1), dimensions={0}, to_apply=%region_4.5 | reduce | flops 458752 | bytes 2359300 | tf_op jit(solution)/shard_map/reduce_sum | solution.py:94
  90.5 0.7 fusion.27
  91.2 0.8 multiply_reduce_fusion
  92.5 0.9 reshape.224
  (189 shorter events, 15.7 us)
Async XLA Ops:
  7.2 81.4 %all-gather.3.cloned.1.call-start = ((), (), s32[]{:S(2)}) async-start(), calls=%async_computation | async-start | bytes 2359296 | tf_op jit(solution)/shard_map/all_gather | solution.py:94
  27.3 4.9 %copy-start.1 = (s32[1,16,32]{2,1,0:T(8,128)S(1)}, s32[1,16,32]{2,1,0:T(8,128)}, u32[]{:S(2)}) copy-start(s32[1,16,32]{2,1,0:T(8,128)} %param.9) | copy-start | bytes 6148
  58.9 0.7 copy-start
Sparse Core Ops, SparseCore 0:
  59.7 28.7 all-gather.2
